TPU v7x, 32 devices: a whole 2x2x4 slice. The times are simulated.
32 devices in a mesh: dp: 8 (over z, core), tp: 4 (over y, x).
Axes of the slice: x: 2, y: 2, z: 4, core: 2. Of those that a mesh axis runs over, the one named last changes fastest.
Arguments:
- tokens: bfloat16 [4096, 4096], P('dp'), may hold values from -6 to 6
- gain: float32 [4096], replicated, may hold values from 0.1 to 1.9
- router: float32 [4096, 8], replicated, may hold values from -0.09375 to 0.09375
- routes: int32 [4096, 2], P('dp'), may hold values from 0 to 7, all different within a row
- w_gate: bfloat16 [2, 4096, 1024], P(None, 'dp', 'tp'), may hold values from -0.125 to 0.125
- w_up: bfloat16 [2, 4096, 1024], P(None, 'dp', 'tp'), may hold values from -0.125 to 0.125
- w_down: bfloat16 [2, 1024, 4096], P(None, 'dp', 'tp'), may hold values from -0.25 to 0.25
Outputs:
- mixed: bfloat16 [4096, 4096], P('dp', 'tp')
Inputs may be any that keep to these rules, and one draw needn't show every extreme that they name: `routes`: each row names two different experts.
All inputs are finite; a program needn't handle non-finite values.
Results may differ from a plain program's by a relative error of at most 0.0065.
Values may be sent and summed in bfloat16 or wider, within the bound.
A program may use at most 64 MiB of HBM per device.

v0:
```python
import jax
import jax.numpy as jnp
from jax import lax
from jax.sharding import PartitionSpec as P

EPS = 1e-06
ROUTE_SCALE = 2.5


def per_device(tokens, gain, router, routes, w_gate, w_up, w_down):
    values = tokens.astype(jnp.float32)
    square = jnp.mean(values * values, axis=-1, keepdims=True)
    normed = (values * lax.rsqrt(square + EPS) * gain).astype(jnp.bfloat16)
    scores = jax.nn.sigmoid(
        jnp.dot(normed.astype(jnp.float32), router, precision=lax.Precision.HIGHEST)
    )
    labels = jnp.arange(router.shape[1], dtype=jnp.int32)
    picked_mask = (routes[:, :, None] == labels[None, None, :]).astype(jnp.float32)
    picked = jnp.sum(picked_mask * scores[:, None, :], axis=-1)
    chosen = jnp.sum(picked_mask, axis=1)
    combine = chosen * scores * ROUTE_SCALE / jnp.sum(picked, axis=-1, keepdims=True)
    held_weights = combine[:, : w_gate.shape[0]]
    full_gate, full_up, full_down = (
        lax.all_gather(w_gate, "dp", axis=1, tiled=True),
        lax.all_gather(w_up, "dp", axis=1, tiled=True),
        lax.all_gather(w_down, "dp", axis=1, tiled=True),
    )
    gate_value = jnp.einsum("td,edf->tef", normed, full_gate, preferred_element_type=jnp.float32)
    up_value = jnp.einsum("td,edf->tef", normed, full_up, preferred_element_type=jnp.float32)
    hidden = (jax.nn.silu(gate_value) * up_value * held_weights[:, :, None]).astype(jnp.bfloat16)
    whole_hidden = lax.all_gather(hidden, "tp", axis=2, tiled=True)
    mixed = jnp.einsum("tef,efd->td", whole_hidden, full_down, preferred_element_type=jnp.float32)
    return mixed.astype(jnp.bfloat16)


def solution(mesh):
    return jax.shard_map(
        per_device,
        mesh=mesh,
        in_specs=(
            P("dp", None),
            P(),
            P(),
            P("dp", None),
            P(None, "dp", "tp"),
            P(None, "dp", "tp"),
            P(None, "dp", "tp"),
        ),
        out_specs=P("dp", "tp"),
        check_vma=False,
    )
```

profile of v0, /device:TPU:0, one launch (start us, length us, event | category | flops | bytes accessed | tf_op | source)
XLA Modules:
  0.0 201.4 jit_solution(2412415738272658088)
XLA Ops:
  6.5 0.0 copy-start
  6.5 0.0 copy-start.3
  6.5 0.0 all-gather.5.cloned.1.call-start
  6.5 0.7 all-gather.5.cloned.1.call-update
  7.3 0.0 all-gather.7.cloned.1.call-start
  7.3 0.7 all-gather.7.cloned.1.call-update
  8.0 0.0 all-gather.11.cloned.1.call-start
  8.1 0.7 all-gather.11.cloned.1.call-update
  8.7 0.0 all-gather.9.cloned.1.call-start
  8.8 0.0 copy-start.1
  8.8 3.2 %fusion = f32[512]{0:T(512)S(1)} fusion(bf16[512,4096]{1,0:T(8,128)(2,1)} %param.7), kind=kLoop, calls=%fused_computation.2 | loop fusion | flops 6290944 | bytes 4196352 | tf_op jit(solution)/shard_map/reduce_sum | solution.py:12
  12.1 0.0 copy-done
  12.1 0.0 copy-done.3
  12.1 0.2 copy-done.1
  12.2 3.4 %fusion.18 = f32[512,8]{0,1:T(8,128)S(1)} fusion(f32[4096,8]{0,1:T(8,128)S(1)} %copy-done, bf16[512,4096]{1,0:T(8,128)(2,1)S(1)} %copy-done.1, f32[4096]{0:T(1024)S(1)} %copy-done.3, f32[512]{0:T(512)S(1)} %add_rsqrt_fusion), kind=kOutput, calls=%fused_computation.16 | convolution fusion | flops 209727488 | bytes 4360192 | tf_op jit(solution)/shard_map/dot_general | solution.py:15
  15.7 0.0 copy-done.2
  15.7 42.8 %all-gather.5.cloned.1.call-done = bf16[2,4096,256]{2,1,0:T(8,128)(2,1)} async-done(((bf16[2,512,256]{2,1,0:T(8,128)(2,1)}), bf16[2,4096,256]{2,1,0:T(8,128)(2,1)}) %all-gather.5.cloned.1.call-update) | async-done | bytes 4194320 | tf_op jit(solution)/shard_map/all_gather | solution.py:24
  58.6 5.8 %fusion.5 = f32[512,2,256]{2,0,1:T(8,128)S(1)} fusion(bf16[2,4096,256]{2,1,0:T(8,128)(2,1)} %all-gather.5.cloned.1.call-done, bf16[512,4096]{1,0:T(8,128)(2,1)} %param.7, f32[4096]{0:T(1024)S(1)} %copy-done.3, f32[512]{0:T(512)S(1)} %add_rsqrt_fusion), kind=kOutput, calls=%fused_computation.7 | convolution fusion | flops 2155872256 | bytes 9455616 | tf_op jit(solution)/shard_map/td,edf->tef/dot_general | solution.py:28
  64.4 41.5 %all-gather.7.cloned.1.call-done = bf16[2,4096,256]{2,1,0:T(8,128)(2,1)} async-done(((bf16[2,512,256]{2,1,0:T(8,128)(2,1)}), bf16[2,4096,256]{2,1,0:T(8,128)(2,1)}) %all-gather.7.cloned.1.call-update) | async-done | bytes 4194320 | tf_op jit(solution)/shard_map/all_gather | solution.py:25
  105.9 6.8 %fusion.13 = bf16[512,2,256]{2,0,1:T(8,128)(2,1)} fusion(bf16[2,4096,256]{2,1,0:T(8,128)(2,1)} %all-gather.7.cloned.1.call-done, f32[512,2,256]{2,0,1:T(8,128)S(1)} %fusion.5, f32[512,2]{0,1:T(2,128)S(1)} %fusion.20, bf16[512,4096]{1,0:T(8,128)(2,1)} %param.7, f32[4096]{0:T(1024)S(1)} %copy-done.3, f32[512]{0:T(512)S(1)} %add_rsqrt_fusion), kind=kOutput, calls=%fused_computation.12 | convolution fusion | flops 2157707264 | bytes 9984000 | tf_op jit(solution)/shard_map/td,edf->tef/dot_general | solution.py:29
  112.6 0.0 all-gather.9.cloned.1.call-update
  112.7 40.5 %all-gather.11.cloned.1.call-done = bf16[2,1024,1024]{2,1,0:T(8,128)(2,1)} async-done(((bf16[2,128,1024]{2,1,0:T(8,128)(2,1)}), bf16[2,1024,1024]{2,1,0:T(8,128)(2,1)}) %all-gather.11.cloned.1.call-update) | async-done | bytes 4194320 | tf_op jit(solution)/shard_map/all_gather | solution.py:26
  153.2 35.6 %all-gather.9.cloned.1.call-done = bf16[512,2,1024]{2,0,1:T(8,128)(2,1)} async-done(((bf16[512,2,256]{2,0,1:T(8,128)(2,1)}), bf16[512,2,1024]{2,0,1:T(8,128)(2,1)}) %all-gather.9.cloned.1.call-update) | async-done | bytes 2097168 | tf_op jit(solution)/shard_map/all_gather | solution.py:31
  188.8 6.1 %bitcast_convert_fusion = bf16[512,1024]{1,0:T(8,128)(2,1)} fusion(bf16[512,2,1024]{2,0,1:T(8,128)(2,1)} %all-gather.9.cloned.1.call-done, bf16[2,1024,1024]{2,1,0:T(8,128)(2,1)} %all-gather.11.cloned.1.call-done), kind=kOutput, calls=%fused_computation.9 | convolution fusion | flops 2148007936 | bytes 7340032 | tf_op jit(solution)/shard_map/tef,efd->td/dot_general | solution.py:32
  (4 shorter events, 0.0 us)
Async XLA Ops:
  6.5 5.5 %copy-start = (f32[4096,8]{0,1:T(8,128)S(1)}, f32[4096,8]{0,1:T(8,128)}, u32[]{:S(2)}) copy-start(f32[4096,8]{0,1:T(8,128)} %param.9) | copy-start | bytes 393220
  6.5 5.5 %copy-start.3 = (f32[4096]{0:T(1024)S(1)}, f32[4096]{0:T(1024)}, u32[]{:S(2)}) copy-start(f32[4096]{0:T(1024)} %param.8) | copy-start | bytes 49156
  6.5 52.0 %all-gather.5.cloned.1.call-start = ((), (), s32[]{:S(2)}) async-start(), calls=%async_computation | async-start | bytes 4718592 | tf_op jit(solution)/shard_map/all_gather | solution.py:24
  7.3 98.6 %all-gather.7.cloned.1.call-start = ((), (), s32[]{:S(2)}) async-start(), calls=%async_computation.1 | async-start | bytes 4718592 | tf_op jit(solution)/shard_map/all_gather | solution.py:25
  8.0 145.2 %all-gather.11.cloned.1.call-start = ((), (), s32[]{:S(2)}) async-start(), calls=%async_computation.3 | async-start | bytes 4718592 | tf_op jit(solution)/shard_map/all_gather | solution.py:26
  8.7 180.0 %all-gather.9.cloned.1.call-start = ((), (), s32[]{:S(2)}) async-start(), calls=%async_computation.2 | async-start | bytes 2621440 | tf_op jit(solution)/shard_map/all_gather | solution.py:31
  8.8 3.5 %copy-start.1 = (bf16[512,4096]{1,0:T(8,128)(2,1)S(1)}, bf16[512,4096]{1,0:T(8,128)(2,1)}, u32[]{:S(2)}) copy-start(bf16[512,4096]{1,0:T(8,128)(2,1)} %param.7) | copy-start | bytes 12582916
  12.0 3.6 %copy-start.2 = (s32[512,2]{0,1:T(2,128)S(1)}, s32[512,2]{0,1:T(2,128)}, u32[]{:S(2)}) copy-start(s32[512,2]{0,1:T(2,128)} %param.10) | copy-start | bytes 12292
Sparse Core Ops, SparseCore 0:
  8.9 49.5 all-gather.4
  60.2 45.6 all-gather.6
  107.5 45.6 all-gather.10
  154.9 33.8 all-gather.8
where the time goes:
time: 202 us; the launch traced here: 201 us
  waiting for transfers between devices  162 us (80%)
  matrix products  22.2 us (11%)
  between operations  13.2 us (7%)
  other arithmetic  3.27 us (2%)
    all_gather x1, waiting for transfers between devices, per_device(): lax.all_gather(w_gate, 'dp', axis=1, tiled=True)  42.8 us
    all_gather x1, waiting for transfers between devices, per_device(): lax.all_gather(w_up, 'dp', axis=1, tiled=True)  41.5 us
    all_gather x1, waiting for transfers between devices, per_device(): lax.all_gather(w_down, 'dp', axis=1, tiled=True)  40.5 us
    all_gather x1, waiting for transfers between devices, per_device(): whole_hidden = lax.all_gather(hidden, 'tp', axis=2, tiled=True)  35.6 us
    dot_general x1, matrix products, per_device(): jnp.einsum('td,edf->tef', normed, full_up, preferred_element_type=jnp.flo...  6.76 us
    dot_general x1, matrix products, per_device(): jnp.einsum('tef,efd->td', whole_hidden, full_down, preferred_element_type...  6.12 us
    dot_general x1, matrix products, per_device(): jnp.einsum('td,edf->tef', normed, full_gate, preferred_element_type=jnp.f...  5.84 us
  transfers between devices with their start and end apart: 4, of which 4 were waited for; matrix products, arithmetic and copies ran while one was open for 10% of the time, Pallas kernels for 0%

commit v1 on v0

--- a/solution.py
+++ b/solution.py
@@ -28,7 +28,12 @@
     gate_value = jnp.einsum("td,edf->tef", normed, full_gate, preferred_element_type=jnp.float32)
     up_value = jnp.einsum("td,edf->tef", normed, full_up, preferred_element_type=jnp.float32)
     hidden = (jax.nn.silu(gate_value) * up_value * held_weights[:, :, None]).astype(jnp.bfloat16)
-    whole_hidden = lax.all_gather(hidden, "tp", axis=2, tiled=True)
+    ring = [hidden]
+    for hop in range(3):
+        ring.append(lax.ppermute(ring[-1], "tp", [(dev, (dev + 1) % 4) for dev in range(4)]))
+    whole_hidden = jnp.roll(
+        jnp.concatenate(ring[::-1], axis=2), (lax.axis_index("tp") + 1) * ring[0].shape[2], axis=2
+    )
     mixed = jnp.einsum("tef,efd->td", whole_hidden, full_down, preferred_element_type=jnp.float32)
     return mixed.astype(jnp.bfloat16)
 

time: 202 us -> 174 us (0.86)
  waiting for transfers between devices: 162 us -> 123 us
  local copies, waits for them, and re-layouts: 0.18 us -> 11 us
  starting transfers between devices: 0.12 us -> 2.17 us
    ppermute x0 -> x3, waiting for transfers between devices: none -> 40.6 us  [per_device(): lax.ppermute(ring[-1], 'tp', [(dev, (dev + 1) % 4) for dev in range(4)])]
    all_gather x1, waiting for transfers between devices: 40.5 us -> 0.01 us  [per_device(): lax.all_gather(w_down, 'dp', axis=1, tiled=True)]
    all_gather x1 -> x0, waiting for transfers between devices: 35.6 us -> none  [per_device(): whole_hidden = lax.all_gather(hidden, 'tp', axis=2, tiled=True)]
    unnamed x8 -> x17, local copies, waits for them, and re-layouts: 0.18 us -> 10.2 us
    all_gather x1, waiting for transfers between devices: 42.8 us -> 40.1 us  [per_device(): lax.all_gather(w_gate, 'dp', axis=1, tiled=True)]
    ppermute x0 -> x3, starting transfers between devices: none -> 2.09 us  [per_device(): lax.ppermute(ring[-1], 'tp', [(dev, (dev + 1) % 4) for dev in range(4)])]
  transfers between devices with their start and end apart: 4 -> 6, of which waited for: 4 -> 5; matrix products, arithmetic and copies ran while one was open for 10% -> 16% of each run, Pallas kernels for 0% -> 0%
where the time goes in v1:
time: 174 us
  waiting for transfers between devices  123 us (71%)
  matrix products  21.5 us (12%)
  between operations  13.2 us (8%)
  local copies, waits for them, and re-layouts  11 us (6%)
  other arithmetic  3.27 us (2%)
  starting transfers between devices  2.17 us (1%)
    all_gather x1, waiting for transfers between devices, per_device(): lax.all_gather(w_up, 'dp', axis=1, tiled=True)  41.4 us
    ppermute x3, waiting for transfers between devices, per_device(): lax.ppermute(ring[-1], 'tp', [(dev, (dev + 1) % 4) for dev in range(4)])  40.6 us
    all_gather x1, waiting for transfers between devices, per_device(): lax.all_gather(w_gate, 'dp', axis=1, tiled=True)  40.1 us
    unnamed x17, local copies, waits for them, and re-layouts  10.2 us
    dot_general x1, matrix products, per_device(): jnp.einsum('tef,efd->td', whole_hidden, full_down, preferred_element_type...  6.14 us
    dot_general x1, matrix products, per_device(): jnp.einsum('td,edf->tef', normed, full_up, preferred_element_type=jnp.flo...  6.04 us
    dot_general x1, matrix products, per_device(): jnp.einsum('td,edf->tef', normed, full_gate, preferred_element_type=jnp.f...  5.91 us
  transfers between devices with their start and end apart: 6, of which 5 were waited for; matrix products, arithmetic and copies ran while one was open for 16% of the time, Pallas kernels for 0%

profile of v1, /device:TPU:0, one launch (start us, length us, event | category | flops | bytes accessed | tf_op | source)
XLA Modules:
  0.0 174.0 jit_solution(8103222563868947899)
XLA Ops:
  6.5 2.1 %copy.13 = bf16[2,512,256]{1,2,0:T(8,128)(2,1)} copy(bf16[2,512,256]{2,1,0:T(8,128)(2,1)} %param.11) | data formatting | bytes 1048576 | tf_op args[4]
  8.7 2.0 %copy.14 = bf16[2,512,256]{1,2,0:T(8,128)(2,1)} copy(bf16[2,512,256]{2,1,0:T(8,128)(2,1)} %param.12) | data formatting | bytes 1048576 | tf_op args[5]
  10.8 0.7 all-gather.8.cloned.1.call-update
  11.5 3.2 %fusion = f32[512]{0:T(512)S(1)} fusion(bf16[512,4096]{1,0:T(8,128)(2,1)} %param.7), kind=kLoop, calls=%fused_computation.2 | loop fusion | flops 6290944 | bytes 4196352 | tf_op jit(solution)/shard_map/reduce_sum | solution.py:12
  14.8 0.2 copy-done.1
  15.0 3.4 %fusion.22 = f32[512,8]{0,1:T(8,128)S(1)} fusion(f32[4096,8]{0,1:T(8,128)S(1)} %copy-done, bf16[512,4096]{1,0:T(8,128)(2,1)S(1)} %copy-done.1, f32[4096]{0:T(1024)S(1)} %copy-done.3, f32[512]{0:T(512)S(1)} %add_rsqrt_fusion), kind=kOutput, calls=%fused_computation.18 | convolution fusion | flops 209727488 | bytes 4360192 | tf_op jit(solution)/shard_map/dot_general | solution.py:15
  18.5 40.1 %all-gather.4.cloned.1.call-done = bf16[2,4096,256]{1,2,0:T(8,128)(2,1)} async-done(((bf16[2,512,256]{1,2,0:T(8,128)(2,1)}), bf16[2,4096,256]{1,2,0:T(8,128)(2,1)}) %all-gather.4.cloned.1.call-update) | async-done | bytes 4194320 | tf_op jit(solution)/shard_map/all_gather | solution.py:24
  58.6 5.9 %fusion.5 = f32[512,2,256]{0,2,1:T(8,128)S(1)} fusion(bf16[2,4096,256]{1,2,0:T(8,128)(2,1)} %all-gather.4.cloned.1.call-done, bf16[512,4096]{1,0:T(8,128)(2,1)} %param.7, f32[4096]{0:T(1024)S(1)} %copy-done.3, f32[512]{0:T(512)S(1)} %add_rsqrt_fusion), kind=kOutput, calls=%fused_computation.7 | convolution fusion | flops 2155872256 | bytes 9455616 | tf_op jit(solution)/shard_map/td,edf->tef/dot_general | solution.py:28
  64.5 41.4 %all-gather.6.cloned.1.call-done = bf16[2,4096,256]{1,2,0:T(8,128)(2,1)} async-done(((bf16[2,512,256]{1,2,0:T(8,128)(2,1)}), bf16[2,4096,256]{1,2,0:T(8,128)(2,1)}) %all-gather.6.cloned.1.call-update) | async-done | bytes 4194320 | tf_op jit(solution)/shard_map/all_gather | solution.py:25
  105.9 6.0 %fusion.17 = bf16[512,2,256]{0,2,1:T(8,128)(2,1)S(1)} fusion(bf16[2,4096,256]{1,2,0:T(8,128)(2,1)} %all-gather.6.cloned.1.call-done, f32[512,2,256]{0,2,1:T(8,128)S(1)} %fusion.5, f32[512,2]{0,1:T(2,128)S(1)} %fusion.24, bf16[512,4096]{1,0:T(8,128)(2,1)} %param.7, f32[4096]{0:T(1024)S(1)} %copy-done.3, f32[512]{0:T(512)S(1)} %add_rsqrt_fusion), kind=kOutput, calls=%fused_computation.14 | convolution fusion | flops 2157707264 | bytes 9984000 | tf_op jit(solution)/shard_map/td,edf->tef/dot_general | solution.py:29
  111.9 1.5 collective-permute-start
  113.4 13.5 %collective-permute-done = bf16[512,2,256]{0,2,1:T(8,128)(2,1)S(1)} collective-permute-done((bf16[512,2,256]{0,2,1:T(8,128)(2,1)S(1)}, bf16[512,2,256]{0,2,1:T(8,128)(2,1)S(1)}, u32[]{:S(2)}, u32[]{:S(2)}) %collective-permute-start) | collective-permute-done | bytes 524320 | tf_op jit(solution)/shard_map/ppermute | solution.py:33
  126.9 0.6 collective-permute-start.1
  127.5 13.6 %collective-permute-done.1 = bf16[512,2,256]{0,2,1:T(8,128)(2,1)S(1)} collective-permute-done((bf16[512,2,256]{0,2,1:T(8,128)(2,1)S(1)}, bf16[512,2,256]{0,2,1:T(8,128)(2,1)S(1)}, u32[]{:S(2)}, u32[]{:S(2)}) %collective-permute-start.1) | collective-permute-done | bytes 524320 | tf_op jit(solution)/shard_map/ppermute | solution.py:33
  141.1 13.4 %collective-permute-done.2 = bf16[512,2,256]{0,2,1:T(8,128)(2,1)S(1)} collective-permute-done((bf16[512,2,256]{0,2,1:T(8,128)(2,1)S(1)}, bf16[512,2,256]{0,2,1:T(8,128)(2,1)S(1)}, u32[]{:S(2)}, u32[]{:S(2)}) %collective-permute-start.2) | collective-permute-done | bytes 524320 | tf_op jit(solution)/shard_map/ppermute | solution.py:33
  154.6 0.8 constant_dynamic-update-slice_fusion.7
  155.4 0.8 constant_dynamic-update-slice_fusion.6
  156.2 0.8 constant_dynamic-update-slice_fusion.5
  157.1 0.9 constant_dynamic-update-slice_fusion.4
  157.9 0.8 constant_dynamic-update-slice_fusion.3
  158.8 0.8 constant_dynamic-update-slice_fusion.2
  159.6 0.8 constant_dynamic-update-slice_fusion.1
  160.4 0.9 constant_dynamic-update-slice_fusion
  161.3 6.1 %bitcast_convert_fusion = bf16[512,1024]{1,0:T(8,128)(2,1)} fusion(bf16[2,1024,1024]{2,1,0:T(8,128)(2,1)} %all-gather.8.cloned.1.call-done, bf16[512,2,2048]{0,2,1:T(8,128)(2,1)} %constant_dynamic-update-slice_fusion, s32[]{:T(128)S(6)} %select_n.14), kind=kOutput, calls=%fused_computation.9 | convolution fusion | flops 2148007936 | bytes 7340036 | tf_op jit(solution)/shard_map/tef,efd->td/dot_general | solution.py:37
  (17 shorter events, 0.2 us)
Async XLA Ops:
  6.5 8.3 %copy-start = (f32[4096,8]{0,1:T(8,128)S(1)}, f32[4096,8]{0,1:T(8,128)}, u32[]{:S(2)}) copy-start(f32[4096,8]{0,1:T(8,128)} %param.9) | copy-start | bytes 393220
  6.5 8.3 %copy-start.3 = (f32[4096]{0:T(1024)S(1)}, f32[4096]{0:T(1024)}, u32[]{:S(2)}) copy-start(f32[4096]{0:T(1024)} %param.8) | copy-start | bytes 49156
  6.5 52.0 %all-gather.4.cloned.1.call-start = ((), (), s32[]{:S(2)}) async-start(), calls=%async_computation | async-start | bytes 4718592 | tf_op jit(solution)/shard_map/all_gather | solution.py:24
  8.7 97.2 %all-gather.6.cloned.1.call-start = ((), (), s32[]{:S(2)}) async-start(), calls=%async_computation.1 | async-start | bytes 4718592 | tf_op jit(solution)/shard_map/all_gather | solution.py:25
  10.8 150.5 %all-gather.8.cloned.1.call-start = ((), (), s32[]{:S(2)}) async-start(), calls=%async_computation.2 | async-start | bytes 4718592 | tf_op jit(solution)/shard_map/all_gather | solution.py:26
  11.5 3.5 %copy-start.1 = (bf16[512,4096]{1,0:T(8,128)(2,1)S(1)}, bf16[512,4096]{1,0:T(8,128)(2,1)}, u32[]{:S(2)}) copy-start(bf16[512,4096]{1,0:T(8,128)(2,1)} %param.7) | copy-start | bytes 12582916
  14.8 3.6 %copy-start.2 = (s32[512,2]{0,1:T(2,128)S(1)}, s32[512,2]{0,1:T(2,128)}, u32[]{:S(2)}) copy-start(s32[512,2]{0,1:T(2,128)} %param.10) | copy-start | bytes 12292
  111.9 15.0 %collective-permute-start = (bf16[512,2,256]{0,2,1:T(8,128)(2,1)S(1)}, bf16[512,2,256]{0,2,1:T(8,128)(2,1)S(1)}, u32[]{:S(2)}, u32[]{:S(2)}) collective-permute-start(bf16[512,2,256]{0,2,1:T(8,128)(2,1)S(1)} %fusion.17), channel_id=1, source_target_pairs={{0,1},{1,2},{2,3},{3,0},{4,5},{5,6},{6,7},{7,4},{8,9},{9,10},{10,1... | collective-permute-start | bytes 1572872 | tf_op jit(solution)/shard_map/ppermute | solution.py:33
  126.9 14.2 %collective-permute-start.1 = (bf16[512,2,256]{0,2,1:T(8,128)(2,1)S(1)}, bf16[512,2,256]{0,2,1:T(8,128)(2,1)S(1)}, u32[]{:S(2)}, u32[]{:S(2)}) collective-permute-start(bf16[512,2,256]{0,2,1:T(8,128)(2,1)S(1)} %collective-permute-done), channel_id=1, source_target_pairs={{0,1},{1,2},{2,3},{3,0},{4,5},{5,6},{6,7},{7,4},{8,9},{9,10},{10,1... | collective-permute-start | bytes 1572872 | tf_op jit(solution)/shard_map/ppermute | solution.py:33
  141.1 13.5 %collective-permute-start.2 = (bf16[512,2,256]{0,2,1:T(8,128)(2,1)S(1)}, bf16[512,2,256]{0,2,1:T(8,128)(2,1)S(1)}, u32[]{:S(2)}, u32[]{:S(2)}) collective-permute-start(bf16[512,2,256]{0,2,1:T(8,128)(2,1)S(1)} %collective-permute-done.1), channel_id=1, source_target_pairs={{0,1},{1,2},{2,3},{3,0},{4,5},{5,6},{6,7},{7,4},{8,9},{9,10},{10,1... | collective-permute-start | bytes 1572872 | tf_op jit(solution)/shard_map/ppermute | solution.py:33
Sparse Core Ops, SparseCore 0:
  8.9 49.5 all-gather.3
  60.2 45.6 all-gather.5
  107.5 45.6 all-gather.7
